TPU v7x, 32 devices: a whole 2x2x4 slice. The times are simulated.
32 devices in a mesh: chan: 8 (over z, y), beam: 4 (over x, core).
Axes of the slice: x: 2, y: 2, z: 4, core: 2. Of those that a mesh axis runs over, the one named last changes fastest.
Arguments:
- signals: bfloat16 [2048, 8192], P('chan', 'beam'), may hold values from -6 to 6
- weights: bfloat16 [3, 2, 512, 2048], P(None, None, 'beam', 'chan'), may hold values from -0.125 to 0.125
- bin_group: int32 [256], replicated, may hold values from 0 to 2
Outputs:
- formed: float32 [256, 2, 512], P('chan', None, 'beam')
All inputs are finite; a program needn't handle non-finite values.
Results may differ from a plain program's by a relative error of at most 0.0042.
Values may be sent and summed in bfloat16 or wider, within the bound.
A program may use at most 64 MiB of HBM per device.

v0:
```python
import math
import jax
import jax.numpy as jnp
from jax import lax
from jax.sharding import PartitionSpec as P


def complex_terms(weight_block, spec_block, onehot):
    selected = onehot[:, :, None, None] * spec_block[:, None, :, :]
    products = jnp.einsum(
        "gpbc,fgqc->fpqb", weight_block, selected, preferred_element_type=jnp.float32
    )
    real_part = products[:, 0, 0] - products[:, 1, 1]
    imag_part = products[:, 0, 1] + products[:, 1, 0]
    return jnp.stack([real_part, imag_part], 1)


def transform(samples, first_sample, span, total_samples, bin_count):
    block = 512
    frequency = jnp.arange(1, bin_count + 1, dtype=jnp.int32)

    def add_block(step, running):
        start = step * block
        piece = lax.dynamic_slice_in_dim(samples, start, block, 1)
        sample_index = first_sample + start + jnp.arange(block, dtype=jnp.int32)
        phases = frequency[:, None] * sample_index[None, :] % total_samples
        angles = 2.0 * math.pi / total_samples * phases.astype(jnp.float32)
        twiddle = jnp.stack([jnp.cos(angles), -jnp.sin(angles)], 1).astype(jnp.bfloat16)
        return running + lax.dot_general(
            twiddle, piece, (((2,), (1,)), ((), ())), preferred_element_type=jnp.float32
        )

    empty = jnp.zeros((bin_count, 2, samples.shape[0]), jnp.float32)
    return lax.fori_loop(0, span // block, add_block, empty)


def shards(signals, weights, bin_group):
    samples_dev = signals.shape[1]
    total_samples = samples_dev * lax.axis_size("beam")
    bin_count = bin_group.shape[0]
    set_count = weights.shape[0]
    scale = 1.0 / math.sqrt(total_samples)
    full_time = lax.all_to_all(signals, "beam", split_axis=0, concat_axis=1, tiled=True)
    partial_value = transform(full_time, 0, total_samples, total_samples, bin_count)
    own_spec = (partial_value * scale).astype(jnp.bfloat16)
    spectrum = lax.all_gather(own_spec, "beam", axis=2, tiled=True)
    bin_dev = bin_count // lax.axis_size("chan")
    set_ids = jnp.arange(set_count, dtype=jnp.int32)
    local_spec = lax.all_to_all(spectrum, "chan", split_axis=0, concat_axis=2, tiled=True)
    local_sets = lax.dynamic_slice_in_dim(bin_group, lax.axis_index("chan") * bin_dev, bin_dev)
    onehot = (local_sets[:, None] == set_ids[None, :]).astype(jnp.bfloat16)
    return complex_terms(lax.all_gather(weights, "chan", axis=3, tiled=True), local_spec, onehot)


def solution(mesh):
    in_specs = (P("chan", "beam"), P(None, None, "beam", "chan"), P())
    out_specs = P("chan", None, "beam")
    return jax.shard_map(shards, mesh=mesh, in_specs=in_specs, out_specs=out_specs, check_vma=False)
```

profile of v0, /device:TPU:0, one launch (start us, length us, event | category | flops | bytes accessed | tf_op | source)
XLA Modules:
  0.0 104.1 jit_solution(7308417566398005931)
XLA Ops:
  6.5 4.2 %all-to-all-start = ((bf16[4,64,2048]{2,1,0:T(8,128)(2,1)}), bf16[4,64,2048]{2,1,0:T(8,128)(2,1)S(1)}, u32[]{:S(2)}, u32[]{:S(2)}) async-start(bf16[4,64,2048]{2,1,0:T(8,128)(2,1)} %bitcast.45), calls=%async_computation | async-start | bytes 2097152 | tf_op jit(solution)/shard_map/all_to_all | solution.py:43
  10.8 1.8 %copy.38 = bf16[3,2,128,256]{3,2,0,1:T(8,128)(2,1)} copy(bf16[3,2,128,256]{3,2,1,0:T(8,128)(2,1)} %param.6) | data formatting | bytes 786432 | tf_op args[1]
  12.6 12.6 %all-to-all-done = bf16[4,64,2048]{2,1,0:T(8,128)(2,1)S(1)} async-done(((bf16[4,64,2048]{2,1,0:T(8,128)(2,1)}), bf16[4,64,2048]{2,1,0:T(8,128)(2,1)S(1)}, u32[]{:S(2)}, u32[]{:S(2)}) %all-to-all-start) | async-done | bytes 1048608 | tf_op jit(solution)/shard_map/all_to_all | solution.py:43
  25.3 45.1 %while.16 = (s32[]{:T(128)}, f32[256,2,64]{0,2,1:T(8,128)S(1)}, bf16[64,8192]{1,0:T(8,128)(2,1)S(1)}, s32[]{:T(128)}, s32[]{:T(128)}, /*index=5*/s32[]{:T(128)}, s32[]{:T(128)}) while((s32[]{:T(128)}, f32[256,2,64]{0,2,1:T(8,128)S(1)}, bf16[64,8192]{1,0:T(8,128)(2,1)S(1)}, s32[]{:T(128)}, s32[]{:T(128)}, /*index=5*/s32[]{:T(128)}, ...), condition=%wide.region_1.2_spmd.clone, body=%wide.region_0.1_spmd.clone.sunk | while | flops 36111112 | bytes 1382549 | solution.py:34
  25.4 2.5 %cosine_convert_fusion.2 = (bf16[256,1,512]{2,0,1:T(8,128)(2,1)S(1)}, bf16[256,1,512]{2,0,1:T(8,128)(2,1)S(1)}) fusion(s32[512]{0:T(512)S(1)} %iota_add_fusion.4, s32[256]{0:T(256)S(1)} %iota_add_fusion.5), kind=kLoop, calls=%fused_computation.14.clone.1 | loop fusion | flops 2228224 | bytes 527360 | tf_op jit(solution)/shard_map/convert
  27.8 0.3 convolution_add_fusion.2
  28.2 2.5 %cosine_convert_fusion.2 = (bf16[256,1,512]{2,0,1:T(8,128)(2,1)S(1)}, bf16[256,1,512]{2,0,1:T(8,128)(2,1)S(1)}) fusion(s32[512]{0:T(512)S(1)} %iota_add_fusion.4, s32[256]{0:T(256)S(1)} %iota_add_fusion.5), kind=kLoop, calls=%fused_computation.14.clone.1 | loop fusion | flops 2228224 | bytes 527360 | tf_op jit(solution)/shard_map/convert
  30.7 0.3 convolution_add_fusion.2
  31.0 2.5 %cosine_convert_fusion.2 = (bf16[256,1,512]{2,0,1:T(8,128)(2,1)S(1)}, bf16[256,1,512]{2,0,1:T(8,128)(2,1)S(1)}) fusion(s32[512]{0:T(512)S(1)} %iota_add_fusion.4, s32[256]{0:T(256)S(1)} %iota_add_fusion.5), kind=kLoop, calls=%fused_computation.14.clone.1 | loop fusion | flops 2228224 | bytes 527360 | tf_op jit(solution)/shard_map/convert
  33.5 0.3 convolution_add_fusion.2
  33.8 2.5 %cosine_convert_fusion.2 = (bf16[256,1,512]{2,0,1:T(8,128)(2,1)S(1)}, bf16[256,1,512]{2,0,1:T(8,128)(2,1)S(1)}) fusion(s32[512]{0:T(512)S(1)} %iota_add_fusion.4, s32[256]{0:T(256)S(1)} %iota_add_fusion.5), kind=kLoop, calls=%fused_computation.14.clone.1 | loop fusion | flops 2228224 | bytes 527360 | tf_op jit(solution)/shard_map/convert
  36.3 0.3 convolution_add_fusion.2
  36.6 2.5 %cosine_convert_fusion.2 = (bf16[256,1,512]{2,0,1:T(8,128)(2,1)S(1)}, bf16[256,1,512]{2,0,1:T(8,128)(2,1)S(1)}) fusion(s32[512]{0:T(512)S(1)} %iota_add_fusion.4, s32[256]{0:T(256)S(1)} %iota_add_fusion.5), kind=kLoop, calls=%fused_computation.14.clone.1 | loop fusion | flops 2228224 | bytes 527360 | tf_op jit(solution)/shard_map/convert
  39.5 2.5 %cosine_convert_fusion.2 = (bf16[256,1,512]{2,0,1:T(8,128)(2,1)S(1)}, bf16[256,1,512]{2,0,1:T(8,128)(2,1)S(1)}) fusion(s32[512]{0:T(512)S(1)} %iota_add_fusion.4, s32[256]{0:T(256)S(1)} %iota_add_fusion.5), kind=kLoop, calls=%fused_computation.14.clone.1 | loop fusion | flops 2228224 | bytes 527360 | tf_op jit(solution)/shard_map/convert
  41.9 0.3 convolution_add_fusion.2
  42.3 2.5 %cosine_convert_fusion.2 = (bf16[256,1,512]{2,0,1:T(8,128)(2,1)S(1)}, bf16[256,1,512]{2,0,1:T(8,128)(2,1)S(1)}) fusion(s32[512]{0:T(512)S(1)} %iota_add_fusion.4, s32[256]{0:T(256)S(1)} %iota_add_fusion.5), kind=kLoop, calls=%fused_computation.14.clone.1 | loop fusion | flops 2228224 | bytes 527360 | tf_op jit(solution)/shard_map/convert
  44.8 0.3 convolution_add_fusion.2
  45.1 2.5 %cosine_convert_fusion.2 = (bf16[256,1,512]{2,0,1:T(8,128)(2,1)S(1)}, bf16[256,1,512]{2,0,1:T(8,128)(2,1)S(1)}) fusion(s32[512]{0:T(512)S(1)} %iota_add_fusion.4, s32[256]{0:T(256)S(1)} %iota_add_fusion.5), kind=kLoop, calls=%fused_computation.14.clone.1 | loop fusion | flops 2228224 | bytes 527360 | tf_op jit(solution)/shard_map/convert
  47.9 2.5 %cosine_convert_fusion.2 = (bf16[256,1,512]{2,0,1:T(8,128)(2,1)S(1)}, bf16[256,1,512]{2,0,1:T(8,128)(2,1)S(1)}) fusion(s32[512]{0:T(512)S(1)} %iota_add_fusion.4, s32[256]{0:T(256)S(1)} %iota_add_fusion.5), kind=kLoop, calls=%fused_computation.14.clone.1 | loop fusion | flops 2228224 | bytes 527360 | tf_op jit(solution)/shard_map/convert
  50.8 2.5 %cosine_convert_fusion.2 = (bf16[256,1,512]{2,0,1:T(8,128)(2,1)S(1)}, bf16[256,1,512]{2,0,1:T(8,128)(2,1)S(1)}) fusion(s32[512]{0:T(512)S(1)} %iota_add_fusion.4, s32[256]{0:T(256)S(1)} %iota_add_fusion.5), kind=kLoop, calls=%fused_computation.14.clone.1 | loop fusion | flops 2228224 | bytes 527360 | tf_op jit(solution)/shard_map/convert
  53.6 2.5 %cosine_convert_fusion.2 = (bf16[256,1,512]{2,0,1:T(8,128)(2,1)S(1)}, bf16[256,1,512]{2,0,1:T(8,128)(2,1)S(1)}) fusion(s32[512]{0:T(512)S(1)} %iota_add_fusion.4, s32[256]{0:T(256)S(1)} %iota_add_fusion.5), kind=kLoop, calls=%fused_computation.14.clone.1 | loop fusion | flops 2228224 | bytes 527360 | tf_op jit(solution)/shard_map/convert
  56.4 2.5 %cosine_convert_fusion.2 = (bf16[256,1,512]{2,0,1:T(8,128)(2,1)S(1)}, bf16[256,1,512]{2,0,1:T(8,128)(2,1)S(1)}) fusion(s32[512]{0:T(512)S(1)} %iota_add_fusion.4, s32[256]{0:T(256)S(1)} %iota_add_fusion.5), kind=kLoop, calls=%fused_computation.14.clone.1 | loop fusion | flops 2228224 | bytes 527360 | tf_op jit(solution)/shard_map/convert
  59.2 2.5 %cosine_convert_fusion.2 = (bf16[256,1,512]{2,0,1:T(8,128)(2,1)S(1)}, bf16[256,1,512]{2,0,1:T(8,128)(2,1)S(1)}) fusion(s32[512]{0:T(512)S(1)} %iota_add_fusion.4, s32[256]{0:T(256)S(1)} %iota_add_fusion.5), kind=kLoop, calls=%fused_computation.14.clone.1 | loop fusion | flops 2228224 | bytes 527360 | tf_op jit(solution)/shard_map/convert
  62.0 2.5 %cosine_convert_fusion.2 = (bf16[256,1,512]{2,0,1:T(8,128)(2,1)S(1)}, bf16[256,1,512]{2,0,1:T(8,128)(2,1)S(1)}) fusion(s32[512]{0:T(512)S(1)} %iota_add_fusion.4, s32[256]{0:T(256)S(1)} %iota_add_fusion.5), kind=kLoop, calls=%fused_computation.14.clone.1 | loop fusion | flops 2228224 | bytes 527360 | tf_op jit(solution)/shard_map/convert
  64.9 2.5 %cosine_convert_fusion.2 = (bf16[256,1,512]{2,0,1:T(8,128)(2,1)S(1)}, bf16[256,1,512]{2,0,1:T(8,128)(2,1)S(1)}) fusion(s32[512]{0:T(512)S(1)} %iota_add_fusion.4, s32[256]{0:T(256)S(1)} %iota_add_fusion.5), kind=kLoop, calls=%fused_computation.14.clone.1 | loop fusion | flops 2228224 | bytes 527360 | tf_op jit(solution)/shard_map/convert
  67.7 2.5 %cosine_convert_fusion.2 = (bf16[256,1,512]{2,0,1:T(8,128)(2,1)S(1)}, bf16[256,1,512]{2,0,1:T(8,128)(2,1)S(1)}) fusion(s32[512]{0:T(512)S(1)} %iota_add_fusion.4, s32[256]{0:T(256)S(1)} %iota_add_fusion.5), kind=kLoop, calls=%fused_computation.14.clone.1 | loop fusion | flops 2228224 | bytes 527360 | tf_op jit(solution)/shard_map/convert
  70.6 5.8 %all_gather.6 = bf16[256,2,256]{0,1,2:T(2,128)(2,1)S(1)} all-gather(bf16[256,2,64]{0,1,2:T(2,128)(2,1)S(1)} %copy.34), channel_id=1, replica_groups=mesh['chan'=8,'beam'=4] {'beam'}, dimensions={2}, use_global_device_ids=true | all-gather | bytes 327680 | tf_op jit(solution)/shard_map/all_gather | solution.py:46
  76.3 1.1 %copy.35 = bf16[256,2,256]{2,1,0:T(2,128)(2,1)} copy(bf16[256,2,256]{0,1,2:T(2,128)(2,1)S(1)} %all_gather.6) | data formatting | bytes 524288 | tf_op jit(solution)/shard_map/all_gather | solution.py:46
  77.5 6.6 %all-to-all-start.1 = ((bf16[256,2,256]{2,1,0:T(2,128)(2,1)}), bf16[256,2,256]{2,1,0:T(2,128)(2,1)S(1)}, u32[]{:S(2)}, u32[]{:S(2)}) async-start(bf16[256,2,256]{2,1,0:T(2,128)(2,1)} %copy.35), calls=%async_computation.1 | async-start | bytes 524288 | tf_op jit(solution)/shard_map/all_to_all | solution.py:49
  84.1 9.3 %all-to-all-done.1 = bf16[256,2,256]{2,1,0:T(2,128)(2,1)S(1)} async-done(((bf16[256,2,256]{2,1,0:T(2,128)(2,1)}), bf16[256,2,256]{2,1,0:T(2,128)(2,1)S(1)}, u32[]{:S(2)}, u32[]{:S(2)}) %all-to-all-start.1) | async-done | bytes 262176 | tf_op jit(solution)/shard_map/all_to_all | solution.py:49
  93.6 3.0 %fusion.14 = f32[32,2,2,128]{3,0,1,2:T(8,128)S(1)} fusion(bf16[3,2,128,2048]{3,2,0,1:T(8,128)(2,1)} %all-gather.2.cloned.1.call-done, bf16[32,2,2048]{2,0,1:T(8,128)(2,1)S(1)} %bitcast.44, bf16[32,3]{0,1:T(4,128)(2,1)S(1)} %fusion.24), kind=kOutput, calls=%fused_computation.23 | convolution fusion | flops 202899456 | bytes 3473600 | tf_op jit(solution)/shard_map/gpbc,fgqc->fpqb/dot_general | solution.py:10
  96.6 0.6 copy.41
  (58 shorter events, 3.5 us)
Async XLA Ops:
  6.5 18.7 %all-to-all-start = ((bf16[4,64,2048]{2,1,0:T(8,128)(2,1)}), bf16[4,64,2048]{2,1,0:T(8,128)(2,1)S(1)}, u32[]{:S(2)}, u32[]{:S(2)}) async-start(bf16[4,64,2048]{2,1,0:T(8,128)(2,1)} %bitcast.45), calls=%async_computation | async-start | bytes 2097152 | tf_op jit(solution)/shard_map/all_to_all | solution.py:43
  10.8 82.8 %all-gather.2.cloned.1.call-start = ((), (), s32[]{:S(2)}) async-start(), calls=%async_computation.2 | async-start | bytes 3538944 | tf_op jit(solution)/shard_map/all_gather | solution.py:52
  25.3 58.7 %copy-start = (s32[256]{0:T(256)S(1)}, s32[256]{0:T(256)}, u32[]{:S(2)}) copy-start(s32[256]{0:T(256)} %param.7) | copy-start | bytes 3076
  77.5 16.0 %all-to-all-start.1 = ((bf16[256,2,256]{2,1,0:T(2,128)(2,1)}), bf16[256,2,256]{2,1,0:T(2,128)(2,1)S(1)}, u32[]{:S(2)}, u32[]{:S(2)}) async-start(bf16[256,2,256]{2,1,0:T(2,128)(2,1)} %copy.35), calls=%async_computation.1 | async-start | bytes 524288 | tf_op jit(solution)/shard_map/all_to_all | solution.py:49
Sparse Core Ops, SparseCore 0:
  13.6 65.2 all-gather.1
where the time goes:
time: 104 us
  other arithmetic  39.5 us (38%)
  waiting for transfers between devices  22 us (21%)
  between operations  13.5 us (13%)
  starting transfers between devices  10.8 us (10%)
  matrix products  7.83 us (8%)
  blocking collectives  5.78 us (6%)
  local copies, waits for them, and re-layouts  3.82 us (4%)
    another operation x16, other arithmetic  39.3 us
    all_to_all x1, waiting for transfers between devices, shards(): lax.all_to_all(signals, 'beam', split_axis=0, concat_axis=1, tiled=True)  12.6 us
    all_to_all x1, waiting for transfers between devices, shards(): lax.all_to_all(spectrum, 'chan', split_axis=0, concat_axis=2, tiled=True)  9.34 us
    all_to_all x1, starting transfers between devices, shards(): lax.all_to_all(spectrum, 'chan', split_axis=0, concat_axis=2, tiled=True)  6.57 us
    all_gather x1, blocking collectives, shards(): spectrum = lax.all_gather(own_spec, 'beam', axis=2, tiled=True)  5.78 us
    dot_general x16, matrix products, add_block(): lax.dot_general(twiddle, piece, (((2,), (1,)), ((), ())), preferred_eleme...  4.86 us
    all_to_all x1, starting transfers between devices, shards(): lax.all_to_all(signals, 'beam', split_axis=0, concat_axis=1, tiled=True)  4.24 us
    dot_general x1, matrix products, complex_terms(): jnp.einsum('gpbc,fgqc->fpqb', weight_block, selected, preferred_element_t...  2.97 us
  transfers between devices with their start and end apart: 3, of which 2 were waited for; matrix products, arithmetic and copies ran while one was open for 46% of the time, Pallas kernels for 0%

commit v1 on v0

--- a/solution.py
+++ b/solution.py
@@ -3,6 +3,13 @@
 import jax.numpy as jnp
 from jax import lax
 from jax.sharding import PartitionSpec as P
+
+
+def try_all_kinds(page, which_axis):
+    everything = lax.axis_size(which_axis)
+    arr_next = jnp.split(page, everything, 0)
+    z1 = lax.all_to_all(jnp.stack(arr_next, axis=0), which_axis, 0, 0)
+    return jnp.concatenate(z1, 2)
 
 
 def complex_terms(weight_block, spec_block, onehot):
@@ -46,7 +53,7 @@
     spectrum = lax.all_gather(own_spec, "beam", axis=2, tiled=True)
     bin_dev = bin_count // lax.axis_size("chan")
     set_ids = jnp.arange(set_count, dtype=jnp.int32)
-    local_spec = lax.all_to_all(spectrum, "chan", split_axis=0, concat_axis=2, tiled=True)
+    local_spec = try_all_kinds(spectrum, "chan")
     local_sets = lax.dynamic_slice_in_dim(bin_group, lax.axis_index("chan") * bin_dev, bin_dev)
     onehot = (local_sets[:, None] == set_ids[None, :]).astype(jnp.bfloat16)
     return complex_terms(lax.all_gather(weights, "chan", axis=3, tiled=True), local_spec, onehot)

time: 104 us -> 110 us (1.058)
  local copies, waits for them, and re-layouts: 3.82 us -> 9.29 us
    unnamed x3 -> x10, local copies, waits for them, and re-layouts: 1.77 us -> 6.08 us
    another operation x0 -> x10, local copies, waits for them, and re-layouts: none -> 2.3 us  [try_all_kinds(): z1 = lax.all_to_all(jnp.stack(arr_next, axis=0), which_axis, 0, 0)]
    all_gather x1 -> x0, local copies, waits for them, and re-layouts: 1.12 us -> none  [shards(): spectrum = lax.all_gather(own_spec, 'beam', axis=2, tiled=True)]
  transfers between devices with their start and end apart: 3 -> 3, of which waited for: 2 -> 2; matrix products, arithmetic and copies ran while one was open for 46% -> 48% of each run, Pallas kernels for 0% -> 0%
where the time goes in v1:
time: 110 us
  other arithmetic  39.5 us (36%)
  waiting for transfers between devices  22 us (20%)
  between operations  13.5 us (12%)
  starting transfers between devices  10.8 us (10%)
  local copies, waits for them, and re-layouts  9.29 us (8%)
  matrix products  7.86 us (7%)
  blocking collectives  5.78 us (5%)
    another operation x16, other arithmetic  39.3 us
    all_to_all x1, waiting for transfers between devices, shards(): lax.all_to_all(signals, 'beam', split_axis=0, concat_axis=1, tiled=True)  12.6 us
    all_to_all x1, waiting for transfers between devices, try_all_kinds(): z1 = lax.all_to_all(jnp.stack(arr_next, axis=0), which_axis, 0, 0)  9.34 us
    all_to_all x1, starting transfers between devices, try_all_kinds(): z1 = lax.all_to_all(jnp.stack(arr_next, axis=0), which_axis, 0, 0)  6.56 us
    unnamed x10, local copies, waits for them, and re-layouts  6.08 us
    all_gather x1, blocking collectives, shards(): spectrum = lax.all_gather(own_spec, 'beam', axis=2, tiled=True)  5.78 us
    dot_general x16, matrix products, add_block(): lax.dot_general(twiddle, piece, (((2,), (1,)), ((), ())), preferred_eleme...  4.88 us
    all_to_all x1, starting transfers between devices, shards(): lax.all_to_all(signals, 'beam', split_axis=0, concat_axis=1, tiled=True)  4.24 us
  transfers between devices with their start and end apart: 3, of which 2 were waited for; matrix products, arithmetic and copies ran while one was open for 48% of the time, Pallas kernels for 0%

profile of v1, /device:TPU:0, one launch (start us, length us, event | category | flops | bytes accessed | tf_op | source)
XLA Modules:
  0.0 109.6 jit_solution(3557003366026695402)
XLA Ops:
  6.5 4.2 %all-to-all-start = ((bf16[4,64,2048]{2,1,0:T(8,128)(2,1)}), bf16[4,64,2048]{2,1,0:T(8,128)(2,1)S(1)}, u32[]{:S(2)}, u32[]{:S(2)}) async-start(bf16[4,64,2048]{2,1,0:T(8,128)(2,1)} %bitcast.59), calls=%async_computation | async-start | bytes 2097152 | tf_op jit(solution)/shard_map/all_to_all | solution.py:50
  10.8 1.8 %copy.54 = bf16[3,2,128,256]{3,2,0,1:T(8,128)(2,1)} copy(bf16[3,2,128,256]{3,2,1,0:T(8,128)(2,1)} %param.6) | data formatting | bytes 786432 | tf_op args[1]
  12.6 12.6 %all-to-all-done = bf16[4,64,2048]{2,1,0:T(8,128)(2,1)S(1)} async-done(((bf16[4,64,2048]{2,1,0:T(8,128)(2,1)}), bf16[4,64,2048]{2,1,0:T(8,128)(2,1)S(1)}, u32[]{:S(2)}, u32[]{:S(2)}) %all-to-all-start) | async-done | bytes 1048608 | tf_op jit(solution)/shard_map/all_to_all | solution.py:50
  25.3 45.2 %while.16 = (s32[]{:T(128)}, f32[256,2,64]{0,2,1:T(8,128)S(1)}, bf16[64,8192]{1,0:T(8,128)(2,1)S(1)}, s32[]{:T(128)}, s32[]{:T(128)}, /*index=5*/s32[]{:T(128)}, s32[]{:T(128)}) while((s32[]{:T(128)}, f32[256,2,64]{0,2,1:T(8,128)S(1)}, bf16[64,8192]{1,0:T(8,128)(2,1)S(1)}, s32[]{:T(128)}, s32[]{:T(128)}, /*index=5*/s32[]{:T(128)}, ...), condition=%wide.region_1.2_spmd.clone, body=%wide.region_0.1_spmd.clone.sunk | while | flops 36111112 | bytes 1382541 | solution.py:41
  25.4 2.5 %cosine_convert_fusion.2 = (bf16[256,1,512]{2,0,1:T(8,128)(2,1)S(1)}, bf16[256,1,512]{2,0,1:T(8,128)(2,1)S(1)}) fusion(s32[512]{0:T(512)S(1)} %iota_add_fusion.4, s32[256]{0:T(256)S(1)} %iota_add_fusion.5), kind=kLoop, calls=%fused_computation.14.clone.1 | loop fusion | flops 2228224 | bytes 527360 | tf_op jit(solution)/shard_map/convert
  28.2 2.5 %cosine_convert_fusion.2 = (bf16[256,1,512]{2,0,1:T(8,128)(2,1)S(1)}, bf16[256,1,512]{2,0,1:T(8,128)(2,1)S(1)}) fusion(s32[512]{0:T(512)S(1)} %iota_add_fusion.4, s32[256]{0:T(256)S(1)} %iota_add_fusion.5), kind=kLoop, calls=%fused_computation.14.clone.1 | loop fusion | flops 2228224 | bytes 527360 | tf_op jit(solution)/shard_map/convert
  31.0 2.5 %cosine_convert_fusion.2 = (bf16[256,1,512]{2,0,1:T(8,128)(2,1)S(1)}, bf16[256,1,512]{2,0,1:T(8,128)(2,1)S(1)}) fusion(s32[512]{0:T(512)S(1)} %iota_add_fusion.4, s32[256]{0:T(256)S(1)} %iota_add_fusion.5), kind=kLoop, calls=%fused_computation.14.clone.1 | loop fusion | flops 2228224 | bytes 527360 | tf_op jit(solution)/shard_map/convert
  33.8 2.5 %cosine_convert_fusion.2 = (bf16[256,1,512]{2,0,1:T(8,128)(2,1)S(1)}, bf16[256,1,512]{2,0,1:T(8,128)(2,1)S(1)}) fusion(s32[512]{0:T(512)S(1)} %iota_add_fusion.4, s32[256]{0:T(256)S(1)} %iota_add_fusion.5), kind=kLoop, calls=%fused_computation.14.clone.1 | loop fusion | flops 2228224 | bytes 527360 | tf_op jit(solution)/shard_map/convert
  36.7 2.5 %cosine_convert_fusion.2 = (bf16[256,1,512]{2,0,1:T(8,128)(2,1)S(1)}, bf16[256,1,512]{2,0,1:T(8,128)(2,1)S(1)}) fusion(s32[512]{0:T(512)S(1)} %iota_add_fusion.4, s32[256]{0:T(256)S(1)} %iota_add_fusion.5), kind=kLoop, calls=%fused_computation.14.clone.1 | loop fusion | flops 2228224 | bytes 527360 | tf_op jit(solution)/shard_map/convert
  39.5 2.5 %cosine_convert_fusion.2 = (bf16[256,1,512]{2,0,1:T(8,128)(2,1)S(1)}, bf16[256,1,512]{2,0,1:T(8,128)(2,1)S(1)}) fusion(s32[512]{0:T(512)S(1)} %iota_add_fusion.4, s32[256]{0:T(256)S(1)} %iota_add_fusion.5), kind=kLoop, calls=%fused_computation.14.clone.1 | loop fusion | flops 2228224 | bytes 527360 | tf_op jit(solution)/shard_map/convert
  42.3 2.5 %cosine_convert_fusion.2 = (bf16[256,1,512]{2,0,1:T(8,128)(2,1)S(1)}, bf16[256,1,512]{2,0,1:T(8,128)(2,1)S(1)}) fusion(s32[512]{0:T(512)S(1)} %iota_add_fusion.4, s32[256]{0:T(256)S(1)} %iota_add_fusion.5), kind=kLoop, calls=%fused_computation.14.clone.1 | loop fusion | flops 2228224 | bytes 527360 | tf_op jit(solution)/shard_map/convert
  45.1 2.5 %cosine_convert_fusion.2 = (bf16[256,1,512]{2,0,1:T(8,128)(2,1)S(1)}, bf16[256,1,512]{2,0,1:T(8,128)(2,1)S(1)}) fusion(s32[512]{0:T(512)S(1)} %iota_add_fusion.4, s32[256]{0:T(256)S(1)} %iota_add_fusion.5), kind=kLoop, calls=%fused_computation.14.clone.1 | loop fusion | flops 2228224 | bytes 527360 | tf_op jit(solution)/shard_map/convert
  48.0 2.5 %cosine_convert_fusion.2 = (bf16[256,1,512]{2,0,1:T(8,128)(2,1)S(1)}, bf16[256,1,512]{2,0,1:T(8,128)(2,1)S(1)}) fusion(s32[512]{0:T(512)S(1)} %iota_add_fusion.4, s32[256]{0:T(256)S(1)} %iota_add_fusion.5), kind=kLoop, calls=%fused_computation.14.clone.1 | loop fusion | flops 2228224 | bytes 527360 | tf_op jit(solution)/shard_map/convert
  50.8 2.5 %cosine_convert_fusion.2 = (bf16[256,1,512]{2,0,1:T(8,128)(2,1)S(1)}, bf16[256,1,512]{2,0,1:T(8,128)(2,1)S(1)}) fusion(s32[512]{0:T(512)S(1)} %iota_add_fusion.4, s32[256]{0:T(256)S(1)} %iota_add_fusion.5), kind=kLoop, calls=%fused_computation.14.clone.1 | loop fusion | flops 2228224 | bytes 527360 | tf_op jit(solution)/shard_map/convert
  53.6 2.5 %cosine_convert_fusion.2 = (bf16[256,1,512]{2,0,1:T(8,128)(2,1)S(1)}, bf16[256,1,512]{2,0,1:T(8,128)(2,1)S(1)}) fusion(s32[512]{0:T(512)S(1)} %iota_add_fusion.4, s32[256]{0:T(256)S(1)} %iota_add_fusion.5), kind=kLoop, calls=%fused_computation.14.clone.1 | loop fusion | flops 2228224 | bytes 527360 | tf_op jit(solution)/shard_map/convert
  56.4 2.5 %cosine_convert_fusion.2 = (bf16[256,1,512]{2,0,1:T(8,128)(2,1)S(1)}, bf16[256,1,512]{2,0,1:T(8,128)(2,1)S(1)}) fusion(s32[512]{0:T(512)S(1)} %iota_add_fusion.4, s32[256]{0:T(256)S(1)} %iota_add_fusion.5), kind=kLoop, calls=%fused_computation.14.clone.1 | loop fusion | flops 2228224 | bytes 527360 | tf_op jit(solution)/shard_map/convert
  59.3 2.5 %cosine_convert_fusion.2 = (bf16[256,1,512]{2,0,1:T(8,128)(2,1)S(1)}, bf16[256,1,512]{2,0,1:T(8,128)(2,1)S(1)}) fusion(s32[512]{0:T(512)S(1)} %iota_add_fusion.4, s32[256]{0:T(256)S(1)} %iota_add_fusion.5), kind=kLoop, calls=%fused_computation.14.clone.1 | loop fusion | flops 2228224 | bytes 527360 | tf_op jit(solution)/shard_map/convert
  62.1 2.5 %cosine_convert_fusion.2 = (bf16[256,1,512]{2,0,1:T(8,128)(2,1)S(1)}, bf16[256,1,512]{2,0,1:T(8,128)(2,1)S(1)}) fusion(s32[512]{0:T(512)S(1)} %iota_add_fusion.4, s32[256]{0:T(256)S(1)} %iota_add_fusion.5), kind=kLoop, calls=%fused_computation.14.clone.1 | loop fusion | flops 2228224 | bytes 527360 | tf_op jit(solution)/shard_map/convert
  64.9 2.5 %cosine_convert_fusion.2 = (bf16[256,1,512]{2,0,1:T(8,128)(2,1)S(1)}, bf16[256,1,512]{2,0,1:T(8,128)(2,1)S(1)}) fusion(s32[512]{0:T(512)S(1)} %iota_add_fusion.4, s32[256]{0:T(256)S(1)} %iota_add_fusion.5), kind=kLoop, calls=%fused_computation.14.clone.1 | loop fusion | flops 2228224 | bytes 527360 | tf_op jit(solution)/shard_map/convert
  67.7 2.5 %cosine_convert_fusion.2 = (bf16[256,1,512]{2,0,1:T(8,128)(2,1)S(1)}, bf16[256,1,512]{2,0,1:T(8,128)(2,1)S(1)}) fusion(s32[512]{0:T(512)S(1)} %iota_add_fusion.4, s32[256]{0:T(256)S(1)} %iota_add_fusion.5), kind=kLoop, calls=%fused_computation.14.clone.1 | loop fusion | flops 2228224 | bytes 527360 | tf_op jit(solution)/shard_map/convert
  70.6 5.8 %all_gather.6 = bf16[256,2,256]{0,1,2:T(2,128)(2,1)S(1)} all-gather(bf16[256,2,64]{0,1,2:T(2,128)(2,1)S(1)} %copy.44), channel_id=1, replica_groups=mesh['chan'=8,'beam'=4] {'beam'}, dimensions={2}, use_global_device_ids=true | all-gather | bytes 327680 | tf_op jit(solution)/shard_map/all_gather | solution.py:53
  76.4 1.0 slice_bitcast_fusion
  78.1 0.6 constant_dynamic-update-slice_fusion.7
  78.8 0.6 constant_dynamic-update-slice_fusion.6
  79.4 0.6 constant_dynamic-update-slice_fusion.5
  80.0 0.6 constant_dynamic-update-slice_fusion.4
  81.2 0.6 constant_dynamic-update-slice_fusion.2
  82.4 0.6 constant_dynamic-update-slice_fusion
  83.0 6.6 %all-to-all-start.1 = ((bf16[8,32,2,256]{3,1,2,0:T(8,128)(2,1)}), bf16[8,32,2,256]{3,1,2,0:T(8,128)(2,1)S(1)}, u32[]{:S(2)}, u32[]{:S(2)}) async-start(bf16[8,32,2,256]{3,1,2,0:T(8,128)(2,1)} %constant_dynamic-update-slice_fusion), calls=%async_computation.1 | async-start | bytes 524288 | tf_op jit(solution)/shard_map/all_to_all | solution.py:11
  89.7 9.3 %all-to-all-done.1 = bf16[8,32,2,256]{3,1,2,0:T(8,128)(2,1)S(1)} async-done(((bf16[8,32,2,256]{3,1,2,0:T(8,128)(2,1)}), bf16[8,32,2,256]{3,1,2,0:T(8,128)(2,1)S(1)}, u32[]{:S(2)}, u32[]{:S(2)}) %all-to-all-start.1) | async-done | bytes 262176 | tf_op jit(solution)/shard_map/all_to_all | solution.py:11
  99.1 3.0 %fusion.14 = f32[32,2,2,128]{3,0,1,2:T(8,128)S(1)} fusion(bf16[3,2,128,2048]{3,2,0,1:T(8,128)(2,1)} %all-gather.2.cloned.1.call-done, bf16[32,2,2048]{2,0,1:T(8,128)(2,1)S(1)} %bitcast.58, bf16[32,3]{0,1:T(4,128)(2,1)S(1)} %fusion.24), kind=kOutput, calls=%fused_computation.23 | convolution fusion | flops 202899456 | bytes 3473600 | tf_op jit(solution)/shard_map/gpbc,fgqc->fpqb/dot_general | solution.py:17
  102.1 0.6 copy.57
  (73 shorter events, 7.2 us)
Async XLA Ops:
  6.5 18.7 %all-to-all-start = ((bf16[4,64,2048]{2,1,0:T(8,128)(2,1)}), bf16[4,64,2048]{2,1,0:T(8,128)(2,1)S(1)}, u32[]{:S(2)}, u32[]{:S(2)}) async-start(bf16[4,64,2048]{2,1,0:T(8,128)(2,1)} %bitcast.59), calls=%async_computation | async-start | bytes 2097152 | tf_op jit(solution)/shard_map/all_to_all | solution.py:50
  10.8 88.3 %all-gather.2.cloned.1.call-start = ((), (), s32[]{:S(2)}) async-start(), calls=%async_computation.2 | async-start | bytes 3538944 | tf_op jit(solution)/shard_map/all_gather | solution.py:59
  70.5 19.1 %copy-start = (s32[256]{0:T(256)S(1)}, s32[256]{0:T(256)}, u32[]{:S(2)}) copy-start(s32[256]{0:T(256)} %param.7) | copy-start | bytes 3076
  83.0 16.0 %all-to-all-start.1 = ((bf16[8,32,2,256]{3,1,2,0:T(8,128)(2,1)}), bf16[8,32,2,256]{3,1,2,0:T(8,128)(2,1)S(1)}, u32[]{:S(2)}, u32[]{:S(2)}) async-start(bf16[8,32,2,256]{3,1,2,0:T(8,128)(2,1)} %constant_dynamic-update-slice_fusion), calls=%async_computation.1 | async-start | bytes 524288 | tf_op jit(solution)/shard_map/all_to_all | solution.py:11
Sparse Core Ops, SparseCore 0:
  13.6 65.2 all-gather.1
